TPU v7x, 128 devices: a whole 4x4x4 slice. The times are simulated.
128 devices in a mesh: seq: 128 (over z, y, x, core).
Axes of the slice: x: 4, y: 4, z: 4, core: 2. Of those that a mesh axis runs over, the one named last changes fastest.
Arguments:
- queries: bfloat16 [2, 4, 128, 576], replicated, may hold values from -40 to 40
- latent_cache: bfloat16 [2, 524288, 576], P(None, 'seq'), may hold values from -6 to 6
- lengths: int32 [2], replicated, may hold values from 65536 to 524288
- offsets: int32 [2, 4], replicated, may hold values from 0 to 3
Outputs:
- attended: bfloat16 [2, 4, 128, 512], replicated
All inputs are finite; a program needn't handle non-finite values.
Results may differ from a plain program's by a relative error of at most 0.001.
The roundings to bfloat16 on the way count: a program that leaves them out, or rounds other values in their place, can miss the bound.
Values may be sent and summed in bfloat16 or wider, within the bound.
No kernel may reach another device: no remote copies, remote signals or barrier semaphores. Data moves between devices by JAX's collectives and lax.ppermute only.
A program may use at most 128 MiB of HBM per device.

v0:
```python
import jax
import jax.numpy as jnp
from jax import lax
from jax.sharding import Mesh
from jax.sharding import PartitionSpec as P

LATENT = 512
SEQ = ("seq_0", "seq_1", "seq_2", "seq_3")


softmax_scale = 192.0 ** (-0.5)


def sent_to_all(array, axis):
    copies = jnp.broadcast_to(array, (lax.axis_size(axis), *array.shape))
    return lax.all_to_all(copies, axis, split_axis=0, concat_axis=0, tiled=True)


def taken_together(array, axis):
    return sent_to_all(array, axis).max(axis=0)


def one_axis_at_a_time(array, axes):
    far, near = axes
    return taken_together(taken_together(array, near), far)


def in_blocks(array, dim, length):
    shape = array.shape
    parts = array.reshape(*shape[:dim], length, shape[dim] // length, *shape[dim + 1 :])
    return jnp.moveaxis(parts, dim, 0)


def sum_at_owner(array, axis, dim):
    parts = in_blocks(array, dim, lax.axis_size(axis))
    arrived = lax.all_to_all(parts, axis, split_axis=0, concat_axis=0, tiled=True)
    return arrived.sum(axis=0)


def summed_rows(array, axes, dim):
    far, near = axes
    own = sum_at_owner(in_blocks(array, dim, lax.axis_size(far)), near, dim + 1)
    return jnp.sum(lax.all_to_all(own, far, 0, 0, tiled=True), axis=0)


def filled_up(lines, length):
    spare = -lines.shape[0] % length
    if not spare:
        return lines
    return jnp.concatenate([lines, jnp.zeros((spare, *lines.shape[1:]), lines.dtype)])


def laid_out(parts, dim):
    shape = list(parts.shape[1:])
    shape[dim] *= parts.shape[0]
    return jnp.moveaxis(parts, 0, dim).reshape(shape)


def whole_of(array, axes, dim):
    far, near = axes
    parts = sent_to_all(sent_to_all(array, far), near)
    return laid_out(parts.swapaxes(0, 1).reshape(-1, *array.shape), dim)


def sum_by_parts(array, axes):
    own = summed_rows(filled_up(array, lax.axis_size(axes[0]) * lax.axis_size(axes[1])), axes, 0)
    whole = whole_of(own, axes, 0)
    return whole[: len(array)].reshape(array.shape)


def in_one(arrays, axis):
    ends = [0]
    for a in arrays:
        ends.append(ends[-1] + a.size)
    total = sum_by_parts(jnp.concatenate([a.ravel() for a in arrays]), axis)
    return tuple((total[b:e].reshape(a.shape) for a, b, e in zip(arrays, ends, ends[1:])))


def block_partial(rows, cache, limit, start):
    score = jnp.dot(rows, cache.T, preferred_element_type=jnp.float32) * softmax_scale
    places = start + jnp.arange(cache.shape[0], dtype=jnp.int32)
    visible = places[None, :] < limit[:, None]
    score = jnp.where(visible, score, -1e30)
    peak = jnp.max(score, axis=1)
    weight = jnp.where(visible, jnp.exp(score - peak[:, None]), 0.0)
    total = jnp.sum(weight, axis=1)
    partial_value = jnp.dot(
        weight.astype(jnp.bfloat16), cache[:, :LATENT], preferred_element_type=jnp.float32
    )
    return (peak, total, partial_value)


def on_device(queries, latent_cache, lengths, offsets):
    requests, qtokens, heads, width = queries.shape
    cache_dev = latent_cache.shape[1]
    start = lax.axis_index(SEQ) * cache_dev
    rows = queries.reshape(requests, qtokens * heads, width)
    limits = jnp.repeat(lengths[:, None] - qtokens + 1 + offsets, heads, axis=1)

    def compute(operands):
        return block_partial(operands[0], operands[1], operands[2], start)

    peak, total, partial_value = jax.vmap(compute)((rows, latent_cache, limits))
    flat_count = requests * qtokens * heads
    peak = peak.reshape(flat_count)
    total = total.reshape(flat_count)
    partial_value = partial_value.reshape(flat_count, LATENT)
    top = one_axis_at_a_time(peak, (("seq_0", "seq_1", "seq_2"), "seq_3"))
    factor = jnp.exp(peak - top)
    upper, lower = in_one(
        (partial_value * factor[:, None], total * factor), (("seq_0", "seq_1", "seq_2"), "seq_3")
    )
    finished = (upper / lower[:, None]).astype(jnp.bfloat16)
    return finished.reshape(requests, qtokens, heads, LATENT)


def solution(mesh):
    torus = Mesh(mesh.devices.reshape(4, 4, 4, 2), ("seq_0", "seq_1", "seq_2", "seq_3"))
    in_specs = (P(), P(None, SEQ, None), P(), P())
    out_specs = P()
    return jax.shard_map(
        on_device, mesh=torus, in_specs=in_specs, out_specs=out_specs, check_vma=False
    )
```

profile of v0, /device:TPU:1, one launch (start us, length us, event | category | flops | bytes accessed | tf_op | source)
XLA Modules:
  0.0 140.0 jit_solution(14213069643066016103)
XLA Ops:
  0.0 0.0 copy-start
  0.0 0.8 broadcast_add_fusion.1
  0.8 0.7 broadcast_add_fusion
  1.5 0.1 broadcast_bitcast_fusion.1
  1.6 0.0 copy-done
  1.6 15.5 %fusion = (f32[2,512]{1,0:T(2,128)S(1)}, f32[2,512,4096]{2,1,0:T(8,128)}) fusion(s32[2,512]{1,0:T(2,128)S(1)} %bitcast.38, s32[4096]{0:T(1024)S(1)} %iota_add_fusion, bf16[2,4096,576]{1,2,0:T(8,128)(2,1)} %param.5, bf16[2,4,128,576]{2,3,1,0:T(8,128)(2,1)S(1)} %copy-done), kind=kOutput, calls=%fused_computation.2 | convolution fusion | flops 4848614400 | bytes 27418624 | tf_op jit(solution)/shard_map/vmap()/dot_general | solution.py:80
  17.1 4.7 %all_to_all.40 = f32[2,1,1024]{2,1,0:T(1,128)S(1)} all-to-all(f32[2,1,1024]{2,1,0:T(1,128)S(1)} %broadcast_in_dim.30), channel_id=1, replica_groups=mesh['seq_0'=4,'seq_1'=4,'seq_2'=4,'seq_3'=2] {'seq_3'}, dimensions={0} | all-to-all | bytes 16384 | tf_op jit(solution)/shard_map/all_to_all | solution.py:16
  21.9 0.8 broadcast_in_dim.31
  22.7 11.4 %all-to-all-start.1 = ((f32[64,1,1024]{2,1,0:T(1,128)}), f32[64,1,1024]{2,1,0:T(1,128)S(1)}, u32[]{:S(2)}, u32[]{:S(2)}) async-start(f32[64,1,1024]{2,1,0:T(1,128)} %broadcast_in_dim.31), calls=%async_computation.1 | async-start | bytes 524288 | tf_op jit(solution)/shard_map/all_to_all | solution.py:16
  34.1 10.6 %fusion.3 = f32[2,512,512]{2,1,0:T(8,128)S(1)} fusion(bf16[2,4096,576]{1,2,0:T(8,128)(2,1)} %param.5, f32[2,512,4096]{2,1,0:T(8,128)} %get-tuple-element.8, f32[2,512]{1,0:T(2,128)S(1)} %get-tuple-element.7, s32[2,512]{1,0:T(2,128)S(1)} %bitcast.39, s32[4096]{0:T(1024)S(1)} %iota_add_fusion), kind=kOutput, calls=%fused_computation.5 | convolution fusion | flops 4320133120 | bytes 27287552 | tf_op jit(solution)/shard_map/vmap()/dot_general | solution.py:87
  44.7 8.3 %fusion.1 = f32[2,512]{1,0:T(2,128)S(1)} fusion(f32[2,512,4096]{2,1,0:T(8,128)} %get-tuple-element.8, f32[2,512]{1,0:T(2,128)S(1)} %get-tuple-element.7, s32[2,512]{1,0:T(2,128)S(1)} %bitcast.40, s32[4096]{0:T(1024)S(1)} %iota_add_fusion), kind=kLoop, calls=%fused_computation.3 | loop fusion | flops 25164800 | bytes 16805888 | tf_op jit(solution)/shard_map/vmap()/reduce_sum | solution.py:86
  53.1 0.5 copy.33
  53.6 0.0 all-to-all-done.1
  53.6 0.2 reduce_max.29
  53.8 0.2 broadcast_bitcast_fusion
  54.1 0.5 copy.35
  54.6 0.3 mul.40
  54.9 1.5 %pad_maximum_fusion = f32[525312]{0:T(1024)} fusion(f32[1024]{0:T(1024)S(1)} %get-tuple-element.5, f32[524288]{0:T(1024)S(1)} %mul.40), kind=kLoop, calls=%fused_computation.12 | loop fusion | flops 525312 | bytes 4202496 | tf_op jit(solution)/shard_map/concatenate | solution.py:75
  56.4 3.6 %reshape_reshape.6 = f32[64,2,4104]{2,1,0:T(2,128)S(1)} reshape(f32[525312]{0:T(1024)} %pad_maximum_fusion) | data formatting | bytes 4202496 | tf_op jit(solution)/shard_map/reshape;reshape | solution.py:30
  60.0 0.1 copy.24
  60.1 5.7 %all_to_all.41 = f32[2,64,4104]{2,1,0:T(8,128)S(1)} all-to-all(f32[2,64,4104]{2,1,0:T(8,128)S(1)} %copy.24), channel_id=1, replica_groups=mesh['seq_0'=4,'seq_1'=4,'seq_2'=4,'seq_3'=2] {'seq_3'}, dimensions={0} | all-to-all | bytes 4202496 | tf_op jit(solution)/shard_map/all_to_all | solution.py:36
  65.9 1.2 reduce_sum.28
  67.1 2.0 %all_to_all.29 = f32[64,1,4104]{2,1,0:T(1,128)S(1)} reshape(f32[64,4104]{1,0:T(8,128)} %reduce_sum.28) | data formatting | bytes 2101248 | tf_op jit(solution)/shard_map/all_to_all | solution.py:43
  69.1 28.1 %all_to_all.42 = f32[64,1,4104]{2,1,0:T(1,128)S(1)} all-to-all(f32[64,1,4104]{2,1,0:T(1,128)S(1)} %all_to_all.29), channel_id=1, replica_groups=mesh['seq_0'=4,'seq_1'=4,'seq_2'=4,'seq_3'=2] {'seq_0','seq_1','seq_2'}, dimensions={0} | all-to-all | bytes 2101248 | tf_op jit(solution)/shard_map/all_to_all | solution.py:43
  97.2 0.7 reduce_sum.29
  97.8 0.6 broadcast_in_dim.32
  98.4 21.4 %all_to_all.43 = f32[64,1,4104]{2,1,0:T(1,128)S(1)} all-to-all(f32[64,1,4104]{2,1,0:T(1,128)S(1)} %broadcast_in_dim.32), channel_id=1, replica_groups=mesh['seq_0'=4,'seq_1'=4,'seq_2'=4,'seq_3'=2] {'seq_0','seq_1','seq_2'}, dimensions={0} | all-to-all | bytes 2101248 | tf_op jit(solution)/shard_map/all_to_all | solution.py:16
  119.8 0.1 copy.45
  119.8 0.1 broadcast_in_dim.33
  120.0 8.2 %all_to_all.44 = f32[2,64,4104]{2,1,0:T(8,128)S(1)} all-to-all(f32[2,64,4104]{2,1,0:T(8,128)S(1)} %broadcast_in_dim.33), channel_id=1, replica_groups=mesh['seq_0'=4,'seq_1'=4,'seq_2'=4,'seq_3'=2] {'seq_3'}, dimensions={0} | all-to-all | bytes 4202496 | tf_op jit(solution)/shard_map/all_to_all | solution.py:16
  128.2 1.7 %copy.25 = f32[64,2,4104]{2,1,0:T(2,128)S(1)} copy(f32[64,2,4104]{2,0,1:T(8,128)S(1)} %bitcast.31) | data formatting | bytes 4202496 | tf_op jit(solution)/shard_map/transpose | solution.py:62
  129.9 3.1 %reshape_reshape.7 = f32[525312]{0:T(1024)} reshape(f32[64,2,4104]{2,1,0:T(2,128)S(1)} %copy.25) | data formatting | bytes 4202496 | tf_op jit(solution)/shard_map/reshape;reshape | solution.py:56
  133.0 3.6 %slice.13 = f32[1026,512]{1,0:T(8,128)} reshape(f32[64,2,4104]{2,1,0:T(2,128)S(1)} %copy.25) | data formatting | bytes 4202496 | tf_op jit(solution)/shard_map/slice | solution.py:76
  136.6 0.7 slice.17
  137.3 2.8 %fusion.11 = bf16[1024,512]{1,0:T(8,128)(2,1)} fusion(f32[1026,512]{1,0:T(8,128)} %slice.13, f32[1024]{0:T(1024)S(1)} %slice.17), kind=kLoop, calls=%fused_computation.14 | loop fusion | flops 1048576 | bytes 3149824 | tf_op jit(solution)/shard_map/convert_element_type | solution.py:113
  (7 shorter events, 0.1 us)
Async XLA Ops:
  0.0 1.6 %copy-start = (bf16[2,4,128,576]{2,3,1,0:T(8,128)(2,1)S(1)}, bf16[2,4,128,576]{2,3,1,0:T(8,128)(2,1)}, u32[]{:S(2)}) copy-start(bf16[2,4,128,576]{2,3,1,0:T(8,128)(2,1)} %param.4) | copy-start | bytes 3538948
  22.7 30.9 %all-to-all-start.1 = ((f32[64,1,1024]{2,1,0:T(1,128)}), f32[64,1,1024]{2,1,0:T(1,128)S(1)}, u32[]{:S(2)}, u32[]{:S(2)}) async-start(f32[64,1,1024]{2,1,0:T(1,128)} %broadcast_in_dim.31), calls=%async_computation.1 | async-start | bytes 524288 | tf_op jit(solution)/shard_map/all_to_all | solution.py:16
where the time goes:
time: 141 us; the launch traced here: 140 us
  blocking collectives  68.2 us (48%)
  matrix products  26.1 us (19%)
  local copies, waits for them, and re-layouts  17.8 us (13%)
  other arithmetic  16.5 us (12%)
  starting transfers between devices  11.4 us (8%)
    all_to_all x3, blocking collectives, sent_to_all(): return lax.all_to_all(copies, axis, split_axis=0, concat_axis=0, tiled=True)  34.4 us
    all_to_all x1, blocking collectives, summed_rows(): return jnp.sum(lax.all_to_all(own, far, 0, 0, tiled=True), axis=0)  28.1 us
    dot_general x1, matrix products, block_partial(): jnp.dot(rows, cache.T, preferred_element_type=jnp.float32) * softmax_scale  15.5 us
    all_to_all x1, starting transfers between devices, sent_to_all(): return lax.all_to_all(copies, axis, split_axis=0, concat_axis=0, tiled=True)  11.4 us
    dot_general x1, matrix products, block_partial(): jnp.dot(weight.astype(jnp.bfloat16), cache[:, :LATENT], preferred_element...  10.6 us
    reduce_sum x1, other arithmetic, block_partial(): total = jnp.sum(weight, axis=1)  8.35 us
    all_to_all x1, blocking collectives, sum_at_owner(): lax.all_to_all(parts, axis, split_axis=0, concat_axis=0, tiled=True)  5.72 us
    slice x2, local copies, waits for them, and re-layouts, in_one(): total[b:e].reshape(a.shape)  4.24 us
  transfers between devices with their start and end apart: 1, of which 0 were waited for; matrix products, arithmetic and copies ran while one was open for 14% of the time, Pallas kernels for 0%

commit v1 on v0

v1 whole, which is shorter than its diff:
```python
import functools

import jax
import jax.numpy as jnp
from jax import lax
from jax.experimental import pallas as pl
from jax.experimental.pallas import tpu as pltpu
from jax.sharding import Mesh
from jax.sharding import PartitionSpec as P

LATENT = 512
CHIPS = ("seq_0", "seq_1", "seq_2")
CORE = "seq_3"
SEQ = (*CHIPS, CORE)
LANES = 128
HIDDEN = -1e30
SCALE = 192.0 ** (-0.5)
LOG2E = 1.4426950408889634
CHUNK = 1024
F32 = jnp.float32
VMEM_LIMIT = 60 * 1024 * 1024
whole = functools.partial(pl.BlockSpec, memory_space=pltpu.VMEM)


def block_partial(lengths, offsets, query_hbm, cache_hbm, out, stats, query, rows_q, keys, score, sems, *, own):
    qtokens, _, heads = query.shape
    rows = qtokens * heads
    positions = keys.shape[1]
    core = lax.axis_index(CORE)
    request = core if own else 1 - core
    start = lax.axis_index(SEQ) * positions

    def key_copy(j):
        part = pl.ds(j * CHUNK, CHUNK)
        return pltpu.make_async_copy(cache_hbm.at[request, :, part], keys.at[:, part], sems.at[j])

    query_copy = pltpu.make_async_copy(query_hbm.at[request], query, sems.at[positions // CHUNK])
    query_copy.start()
    for j in range(positions // CHUNK):
        key_copy(j).start()
    stats[...] = jnp.full((rows, LANES), HIDDEN, F32)
    lane = lax.broadcasted_iota(jnp.int32, (heads, CHUNK), 1)
    query_copy.wait()
    for t in range(qtokens):
        rows_q[t * heads : (t + 1) * heads, :] = query[t].T

    for j in range(positions // CHUNK):
        part = slice(j * CHUNK, (j + 1) * CHUNK)
        key_copy(j).wait()
        product = jnp.dot(rows_q[:, :LATENT], keys[:LATENT, part], preferred_element_type=F32)
        product += jnp.dot(rows_q[:, LATENT:], keys[LATENT:, part], preferred_element_type=F32)
        for t in range(qtokens):
            r = slice(t * heads, (t + 1) * heads)
            limit = lengths[request] - qtokens + 1 + offsets[request, t] - start
            seen = jnp.where(lane < limit - j * CHUNK, product[r], HIDDEN)
            score[r, part] = seen
            top = stats[r, :]
            for u in range(CHUNK // LANES):
                top = jnp.maximum(top, seen[:, u * LANES : (u + 1) * LANES])
            stats[r, :] = top

    peak = jnp.max(stats[...], axis=1, keepdims=True)
    base = jnp.where(peak < 0.1 * HIDDEN, 0.0, peak)
    total = jnp.zeros((rows, LANES), F32)
    for j in range(positions // CHUNK):
        part = slice(j * CHUNK, (j + 1) * CHUNK)
        weight = jnp.exp2((score[:, part] - base) * (SCALE * LOG2E))
        for u in range(CHUNK // LANES):
            total = total + weight[:, u * LANES : (u + 1) * LANES]
        value = lax.dot_general(
            weight.astype(jnp.bfloat16),
            keys[:LATENT, part],
            (((1,), (1,)), ((), ())),
            preferred_element_type=F32,
        )
        if j == 0:
            out[...] = value
        else:
            out[...] += value
    total = jnp.sum(total, axis=1, keepdims=True)
    left = lax.broadcasted_iota(jnp.int32, (rows, LANES), 1) < LANES // 2
    stats[...] = jnp.where(left, peak, total)


def partials(lengths, offsets, query, cache, own):
    _, qtokens, width, heads = query.shape
    positions = cache.shape[2]
    rows = qtokens * heads
    scalars = pl.BlockSpec(memory_space=pltpu.SMEM)
    arrays = pl.BlockSpec(memory_space=pl.ANY)
    return pl.pallas_call(
        functools.partial(block_partial, own=own),
        in_specs=[scalars, scalars, arrays, arrays],
        out_specs=[whole(), whole()],
        out_shape=[
            jax.ShapeDtypeStruct((rows, LATENT), F32),
            jax.ShapeDtypeStruct((rows, LANES), F32),
        ],
        scratch_shapes=[
            pltpu.VMEM((qtokens, width, heads), jnp.bfloat16),
            pltpu.VMEM((rows, width), jnp.bfloat16),
            pltpu.VMEM((width, positions), jnp.bfloat16),
            pltpu.VMEM((rows, positions), F32),
            pltpu.SemaphoreType.DMA((positions // CHUNK + 1,)),
        ],
        compiler_params=pltpu.CompilerParams(vmem_limit_bytes=VMEM_LIMIT),
        cost_estimate=pl.CostEstimate(
            flops=2 * rows * positions * (width + LATENT),
            bytes_accessed=2 * positions * width,
            transcendentals=rows * positions,
        ),
        name="block_partial",
    )(lengths, offsets, query, cache)


def merge(out_a, stats_a, out_b, stats_b, packed):
    peak_a, total_a = stats_a[:, :1], stats_a[:, LANES // 2 : LANES // 2 + 1]
    peak_b, total_b = stats_b[:, :1], stats_b[:, LANES // 2 : LANES // 2 + 1]
    peak = jnp.maximum(peak_a, peak_b)
    factor_a = jnp.exp2((peak_a - peak) * (SCALE * LOG2E))
    factor_b = jnp.exp2((peak_b - peak) * (SCALE * LOG2E))
    packed[:, :LATENT] = factor_a * out_a[...] + factor_b * out_b[...]
    total = factor_a * total_a + factor_b * total_b
    left = lax.broadcasted_iota(jnp.int32, stats_a.shape, 1) < LANES // 2
    packed[:, LATENT:] = jnp.where(left, peak, total)


def finish(packed, copies):
    chips = packed.shape[0]
    stats = packed[:, :, LATENT:]
    peaks, totals = stats[:, :, :1], stats[:, :, LANES // 2 : LANES // 2 + 1]
    factor = jnp.exp2((peaks - jnp.max(peaks, axis=0, keepdims=True)) * (SCALE * LOG2E))
    lower = jnp.sum(factor * totals, axis=0)
    upper = jnp.sum(factor * packed[:, :, :LATENT], axis=0)
    rows = (upper / lower).astype(jnp.bfloat16)
    copies[...] = jnp.broadcast_to(rows[None], (chips, *rows.shape))


def on_device(queries, latent_cache, lengths, offsets):
    requests, qtokens, heads, width = queries.shape
    rows = qtokens * heads
    chips = lax.axis_size(CHIPS)
    query = jnp.transpose(queries, (0, 1, 3, 2))
    cache = jnp.transpose(latent_cache, (0, 2, 1))
    swap = [(0, 1), (1, 0)]

    lent = partials(lengths, offsets, query, cache, False)
    lent = [lax.ppermute(a, CORE, swap) for a in lent]
    kept = partials(lengths, offsets, query, cache, True)
    packed = pl.pallas_call(
        merge,
        in_specs=[whole()] * 4,
        out_specs=whole(),
        out_shape=jax.ShapeDtypeStruct((rows, LATENT + LANES), F32),
        name="merge",
    )(*kept, *lent)
    packed = packed.reshape(chips, rows // chips, LATENT + LANES)
    packed = lax.all_to_all(packed, CHIPS, 0, 0, tiled=True)
    copies = pl.pallas_call(
        finish,
        in_specs=[whole()],
        out_specs=whole(),
        out_shape=jax.ShapeDtypeStruct((chips, rows // chips, LATENT), jnp.bfloat16),
        name="finish",
    )(packed)
    mine = lax.all_to_all(copies, CHIPS, 0, 0, tiled=True).reshape(rows, LATENT)
    other = lax.ppermute(mine, CORE, swap)
    first = lax.axis_index(CORE) == 0
    both = jnp.where(first, jnp.stack([mine, other]), jnp.stack([other, mine]))
    return both.reshape(requests, qtokens, heads, LATENT)


def solution(mesh):
    torus = Mesh(mesh.devices.reshape(4, 4, 4, 2), SEQ)
    in_specs = (P(), P(None, SEQ, None), P(), P())
    return jax.shard_map(
        on_device, mesh=torus, in_specs=in_specs, out_specs=P(), check_vma=False
    )
```

time: 141 us -> 83.8 us (0.59)
  Pallas kernels: 0 us -> 26.2 us
  matrix products: 26.1 us -> 0 us
  blocking collectives: 68.2 us -> 49.2 us
  local copies, waits for them, and re-layouts: 17.8 us -> 1.03 us
  other arithmetic: 16.5 us -> 1.13 us
  starting transfers between devices: 11.4 us -> 4.21 us
  waiting for transfers between devices: 0.01 us -> 1.54 us
    pallas_call x0 -> x4, Pallas kernels: none -> 26.2 us  [the longest x2 20.6 us: partials(): pl.pallas_call(functools.partial(block_partial, own=own), in_specs=[scala...]
    dot_general x2 -> x0, matrix products: 26.1 us -> none  [the longest x1 15.5 us: block_partial(): jnp.dot(rows, cache.T, preferred_element_type=jnp.float32) * softmax_scale]
    all_to_all x5 -> x2, blocking collectives: 68.2 us -> 49.2 us  [the longest x1 32.2 us: on_device(): packed = lax.all_to_all(packed, CHIPS, 0, 0, tiled=True)]
    all_to_all x1 -> x0, starting transfers between devices: 11.4 us -> none  [sent_to_all(): return lax.all_to_all(copies, axis, split_axis=0, concat_axis=0, tiled=True)]
    reduce_sum x3 -> x0, other arithmetic: 10.2 us -> none  [the longest x1 8.35 us: block_partial(): total = jnp.sum(weight, axis=1)]
    another operation x2 -> x0, local copies, waits for them, and re-layouts: 6.74 us -> none  [the longest x1 3.62 us: in_blocks(): array.reshape(*shape[:dim], length, shape[dim] // length, *shape[dim + 1:])]
    slice x2 -> x0, local copies, waits for them, and re-layouts: 4.24 us -> none  [in_one(): total[b:e].reshape(a.shape)]
    ppermute x0 -> x3, starting transfers between devices: none -> 4.21 us  [the longest x1 2.48 us: on_device(): other = lax.ppermute(mine, CORE, swap)]
  transfers between devices with their start and end apart: 1 -> 3, of which waited for: 0 -> 1; matrix products, arithmetic and copies ran while one was open for 14% -> 0% of each run, Pallas kernels for 0% -> 12%
where the time goes in v1:
time: 83.8 us; the launch traced here: 83.4 us
  blocking collectives  49.2 us (59%)
  Pallas kernels  26.2 us (31%)
  starting transfers between devices  4.21 us (5%)
  waiting for transfers between devices  1.54 us (2%)
  other arithmetic  1.13 us (1%)
  local copies, waits for them, and re-layouts  1.03 us (1%)
    all_to_all x1, blocking collectives, on_device(): packed = lax.all_to_all(packed, CHIPS, 0, 0, tiled=True)  32.2 us
    pallas_call x2, Pallas kernels, partials(): pl.pallas_call(functools.partial(block_partial, own=own), in_specs=[scala...  20.6 us
    all_to_all x1, blocking collectives, on_device(): mine = lax.all_to_all(copies, CHIPS, 0, 0, tiled=True).reshape(rows, LATENT)  17 us
    pallas_call x1, Pallas kernels, on_device(): pl.pallas_call(merge, in_specs=[whole()] * 4, out_specs=whole(), out_shap...  3.29 us
    ppermute x1, starting transfers between devices, on_device(): other = lax.ppermute(mine, CORE, swap)  2.48 us
    pallas_call x1, Pallas kernels, on_device(): pl.pallas_call(finish, in_specs=[whole()], out_specs=whole(), out_shape=j...  2.36 us
    ppermute x2, starting transfers between devices, on_device(): lent = [lax.ppermute(a, CORE, swap) for a in lent]  1.73 us
  transfers between devices with their start and end apart: 3, of which 1 were waited for; matrix products, arithmetic and copies ran while one was open for 0% of the time, Pallas kernels for 12%

profile of v1, /device:TPU:1, one launch (start us, length us, event | category | flops | bytes accessed | tf_op | source)
XLA Modules:
  0.0 83.4 jit_solution(1385669977488851633)
XLA Ops:
  0.0 10.3 %block_partial.3 = (f32[512,512]{1,0:T(8,128)}, f32[512,128]{1,0:T(8,128)}) custom-call(s32[2]{0:T(128)} %lengths.3, s32[2,4]{1,0:T(2,128)} %offsets.3, bf16[2,4,576,128]{3,2,1,0:T(8,128)(2,1)} %bitcast.12, bf16[2,576,4096]{2,1,0:T(8,128)(2,1)} %bitcast.10), custom_call_target="tpu_custom_call" | custom-call | flops 4563402752 | bytes 4718592 | tf_op jit(solution)/shard_map/block_partial/pallas_call | solution.py:91
  10.3 1.5 %collective-permute-start = (f32[512,512]{1,0:T(8,128)}, f32[512,512]{1,0:T(8,128)S(1)}, u32[]{:S(2)}, u32[]{:S(2)}) collective-permute-start(f32[512,512]{1,0:T(8,128)} %get-tuple-element.11), channel_id=1, source_target_pairs={{0,1},{1,0},{2,3},{3,2},{4,5},{5,4},{6,7},{7,6},{8,9},{9,8},{10,11... | collective-permute-start | bytes 3145736 | tf_op jit(solution)/shard_map/ppermute | solution.py:148
  11.8 0.3 collective-permute-start.1
  12.0 10.3 %block_partial.2 = (f32[512,512]{1,0:T(8,128)}, f32[512,128]{1,0:T(8,128)}) custom-call(s32[2]{0:T(128)} %lengths.3, s32[2,4]{1,0:T(2,128)} %offsets.3, bf16[2,4,576,128]{3,2,1,0:T(8,128)(2,1)} %bitcast.13, bf16[2,576,4096]{2,1,0:T(8,128)(2,1)} %bitcast.11), custom_call_target="tpu_custom_call" | custom-call | flops 4563402752 | bytes 4718592 | tf_op jit(solution)/shard_map/block_partial/pallas_call | solution.py:91
  22.3 0.0 collective-permute-done.1.stats_b
  22.3 0.0 copy-start.1
  22.3 0.0 collective-permute-done.out_b
  22.3 0.0 copy-start
  22.4 0.7 copy-done.1
  23.0 0.4 copy-done
  23.4 3.3 %merge.1 = f32[512,640]{1,0:T(8,128)} custom-call(f32[512,512]{1,0:T(8,128)} %get-tuple-element.9.out_a, f32[512,128]{1,0:T(8,128)} %get-tuple-element.10.stats_a, f32[512,512]{1,0:T(8,128)} %copy-done, f32[512,128]{1,0:T(8,128)} %copy-done.1), custom_call_target="tpu_custom_call" | custom-call | tf_op jit(solution)/shard_map/merge/pallas_call | solution.py:150
  26.7 32.2 %all_to_all.10.packed = f32[64,8,640]{2,1,0:T(8,128)} all-to-all(f32[64,8,640]{2,1,0:T(8,128)} %bitcast.6), channel_id=1, replica_groups=mesh['seq_0'=4,'seq_1'=4,'seq_2'=4,'seq_3'=2] {'seq_0','seq_1','seq_2'}, dimensions={0} | all-to-all | bytes 2621440 | tf_op jit(solution)/shard_map/all_to_all | solution.py:158
  58.9 2.4 %finish.1 = bf16[64,8,512]{2,1,0:T(8,128)(2,1)} custom-call(f32[64,8,640]{2,1,0:T(8,128)} %all_to_all.10.packed), custom_call_target="tpu_custom_call" | custom-call | tf_op jit(solution)/shard_map/finish/pallas_call | solution.py:159
  61.3 17.0 %all_to_all.11 = bf16[64,8,512]{2,1,0:T(8,128)(2,1)S(1)} all-to-all(bf16[64,8,512]{2,1,0:T(8,128)(2,1)} %finish.1), channel_id=1, replica_groups=mesh['seq_0'=4,'seq_1'=4,'seq_2'=4,'seq_3'=2] {'seq_0','seq_1','seq_2'}, dimensions={0} | all-to-all | bytes 1048576 | tf_op jit(solution)/shard_map/all_to_all | solution.py:166
  78.3 2.5 %collective-permute-start.2 = (bf16[512,512]{1,0:T(8,128)(2,1)S(1)}, bf16[512,512]{1,0:T(8,128)(2,1)S(1)}, u32[]{:S(2)}, u32[]{:S(2)}) collective-permute-start(bf16[512,512]{1,0:T(8,128)(2,1)S(1)} %bitcast.7), channel_id=1, source_target_pairs={{0,1},{1,0},{2,3},{3,2},{4,5},{5,4},{6,7},{7,6},{8,9},{9,8},{10,11... | collective-permute-start | bytes 1572872 | tf_op jit(solution)/shard_map/ppermute | solution.py:167
  80.8 1.5 %collective-permute-done.2 = bf16[512,512]{1,0:T(8,128)(2,1)S(1)} collective-permute-done((bf16[512,512]{1,0:T(8,128)(2,1)S(1)}, bf16[512,512]{1,0:T(8,128)(2,1)S(1)}, u32[]{:S(2)}, u32[]{:S(2)}) %collective-permute-start.2) | collective-permute-done | bytes 524320 | tf_op jit(solution)/shard_map/ppermute | solution.py:167
  82.3 1.1 %maximum_select_fusion = bf16[2,4,128,512]{3,2,1,0:T(8,128)(2,1)} fusion(bf16[1,4,128,512]{3,2,1,0:T(8,128)(2,1)S(1)} %bitcast.9, bf16[1,4,128,512]{3,2,1,0:T(8,128)(2,1)S(1)} %bitcast.8, pred[]{:T(512)S(6)} %eq.3), kind=kLoop, calls=%fused_computation | loop fusion | flops 1572864 | bytes 2097153 | tf_op jit(solution)/shard_map/jit(_where)/select_n | solution.py:169
Async XLA Ops:
  10.3 12.0 %collective-permute-start = (f32[512,512]{1,0:T(8,128)}, f32[512,512]{1,0:T(8,128)S(1)}, u32[]{:S(2)}, u32[]{:S(2)}) collective-permute-start(f32[512,512]{1,0:T(8,128)} %get-tuple-element.11), channel_id=1, source_target_pairs={{0,1},{1,0},{2,3},{3,2},{4,5},{5,4},{6,7},{7,6},{8,9},{9,8},{10,11... | collective-permute-start | bytes 3145736 | tf_op jit(solution)/shard_map/ppermute | solution.py:148
  11.8 10.6 %collective-permute-start.1 = (f32[512,128]{1,0:T(8,128)}, f32[512,128]{1,0:T(8,128)S(1)}, u32[]{:S(2)}, u32[]{:S(2)}) collective-permute-start(f32[512,128]{1,0:T(8,128)} %get-tuple-element.12), channel_id=1, source_target_pairs={{0,1},{1,0},{2,3},{3,2},{4,5},{5,4},{6,7},{7,6},{8,9},{9,8},{10,11... | collective-permute-start | bytes 786440 | tf_op jit(solution)/shard_map/ppermute | solution.py:148
  22.3 0.7 copy-start.1
  22.3 1.0 %copy-start = (f32[512,512]{1,0:T(8,128)}, f32[512,512]{1,0:T(8,128)S(1)}, u32[]{:S(2)}) copy-start(f32[512,512]{1,0:T(8,128)S(1)} %collective-permute-done.out_b) | copy-start | bytes 3145732
  78.3 4.0 %collective-permute-start.2 = (bf16[512,512]{1,0:T(8,128)(2,1)S(1)}, bf16[512,512]{1,0:T(8,128)(2,1)S(1)}, u32[]{:S(2)}, u32[]{:S(2)}) collective-permute-start(bf16[512,512]{1,0:T(8,128)(2,1)S(1)} %bitcast.7), channel_id=1, source_target_pairs={{0,1},{1,0},{2,3},{3,2},{4,5},{5,4},{6,7},{7,6},{8,9},{9,8},{10,11... | collective-permute-start | bytes 1572872 | tf_op jit(solution)/shard_map/ppermute | solution.py:167

commit v2 on v1

v2 whole, which is shorter than its diff:
```python
import functools

import jax
import jax.numpy as jnp
from jax import lax
from jax.experimental import pallas as pl
from jax.experimental.pallas import tpu as pltpu
from jax.sharding import Mesh
from jax.sharding import PartitionSpec as P

LATENT = 512
CHIPS = ("seq_0", "seq_1", "seq_2")
CORE = "seq_3"
SEQ = (*CHIPS, CORE)
LANES = 128
HIDDEN = -1e30
LOG2_SCALE = 192.0 ** (-0.5) * 1.4426950408889634
CHUNK = 1024
STEPS = 32000.0
FINE = 32768.0
F32 = jnp.float32
whole = functools.partial(pl.BlockSpec, memory_space=pltpu.VMEM)
anywhere = functools.partial(pl.BlockSpec, memory_space=pltpu.HBM)


def attend(request, limits, rows_q, keys, score, triple, ready):
    lengths, offsets = limits
    rows, positions = score.shape
    qtokens = offsets.shape[1]
    heads = rows // qtokens
    start = lax.axis_index(SEQ) * positions
    lane = lax.broadcasted_iota(jnp.int32, (heads, CHUNK), 1)
    stats = triple.at[:, LATENT:]
    stats[...] = jnp.full((rows, LANES), HIDDEN, F32)
    for j in range(positions // CHUNK):
        part = slice(j * CHUNK, (j + 1) * CHUNK)
        ready(j)
        product = jnp.dot(rows_q[:, :LATENT], keys[:LATENT, part], preferred_element_type=F32)
        product += jnp.dot(rows_q[:, LATENT:], keys[LATENT:, part], preferred_element_type=F32)
        for t in range(qtokens):
            r = slice(t * heads, (t + 1) * heads)
            limit = lengths[request] - qtokens + 1 + offsets[request, t] - start
            seen = jnp.where(lane < limit - j * CHUNK, product[r], HIDDEN)
            score[r, part] = seen
            top = stats[r, :]
            for u in range(CHUNK // LANES):
                top = jnp.maximum(top, seen[:, u * LANES : (u + 1) * LANES])
            stats[r, :] = top

    peak = jnp.max(stats[...], axis=1, keepdims=True)
    base = jnp.where(peak < 0.1 * HIDDEN, 0.0, peak)
    total = jnp.zeros((rows, LANES), F32)
    for j in range(positions // CHUNK):
        part = slice(j * CHUNK, (j + 1) * CHUNK)
        weight = jnp.exp2((score[:, part] - base) * LOG2_SCALE)
        for u in range(CHUNK // LANES):
            total = total + weight[:, u * LANES : (u + 1) * LANES]
        value = lax.dot_general(
            weight.astype(jnp.bfloat16),
            keys[:LATENT, part],
            (((1,), (1,)), ((), ())),
            preferred_element_type=F32,
        )
        if j == 0:
            triple[:, :LATENT] = value
        else:
            triple[:, :LATENT] += value
    total = jnp.sum(total, axis=1, keepdims=True)
    left = lax.broadcasted_iota(jnp.int32, (rows, LANES), 1) < LANES // 2
    stats[...] = jnp.where(left, peak, total)


def scalar_copies(arrays, refs, sems):
    return [pltpu.make_async_copy(a, r, sems.at[i]) for i, (a, r) in enumerate(zip(arrays, refs))]


def lend(lengths, offsets, queries, cache, triple, next_q, next_keys, query, rows_q, keys, score, lens, offs, sems, key_sems, next_sems):
    positions = keys.shape[1]
    qtokens, _, heads = query.shape[1:]
    core = lax.axis_index(CORE)
    scalars = scalar_copies((lengths, offsets), (lens, offs), sems)
    query_copy = pltpu.make_async_copy(queries, query, sems.at[2])

    def key_copy(request, into, own_sems, j):
        part = pl.ds(j * CHUNK, CHUNK)
        return pltpu.make_async_copy(cache.at[request, :, part], into.at[:, part], own_sems.at[j])

    parts = range(positions // CHUNK)
    first = [key_copy(1 - core, keys, key_sems, j) for j in parts]
    later = [key_copy(core, next_keys, next_sems, j) for j in parts]
    query_copy.start()
    for copy in (*scalars, *first, *later):
        copy.start()
    query_copy.wait()
    for t in range(qtokens):
        rows_q[t * heads : (t + 1) * heads, :] = query[1 - core, t].T
        next_q[t * heads : (t + 1) * heads, :] = query[core, t].T
    for copy in scalars:
        copy.wait()
    attend(1 - core, (lens, offs), rows_q, keys, score, triple, lambda j: first[j].wait())
    for copy in later:
        copy.wait()


def keep(lengths, offsets, rows_q, keys, triple, score, lens, offs, sems):
    scalars = scalar_copies((lengths, offsets), (lens, offs), sems)
    for copy in scalars:
        copy.start()
    for copy in scalars:
        copy.wait()
    attend(lax.axis_index(CORE), (lens, offs), rows_q, keys, score, triple, lambda j: None)


def in_parts(x):
    whole_part = jnp.round(x)
    rest = (x - whole_part) * FINE
    middle = jnp.round(rest)
    return [whole_part, middle, jnp.round((rest - middle) * FINE)]


def from_parts(stats, at):
    a, b, c = (stats[..., at + i : at + i + 1] for i in range(3))
    return a + (b + c * (1.0 / FINE)) * (1.0 / FINE)


def merge(kept, lent, packed):
    half = LATENT + LANES // 2
    peak_a, peak_b = kept[:, LATENT : LATENT + 1], lent[:, LATENT : LATENT + 1]
    peak = jnp.maximum(peak_a, peak_b)
    factor_a = jnp.exp2((peak_a - peak) * LOG2_SCALE)
    factor_b = jnp.exp2((peak_b - peak) * LOG2_SCALE)
    total = factor_a * kept[:, half : half + 1] + factor_b * lent[:, half : half + 1]
    values = factor_a * kept[:, :LATENT] + factor_b * lent[:, :LATENT]
    largest = jnp.max(jnp.abs(values), axis=1, keepdims=True)
    largest = jnp.where(largest > 0.0, largest, 1.0)
    packed[:, :LATENT] = jnp.round(values * (STEPS / largest)).astype(jnp.int32).astype(jnp.int16)
    level = jnp.maximum(peak * LOG2_SCALE, -STEPS)
    numbers = [*in_parts(level), *in_parts(total), *in_parts(jnp.log2(largest))]
    lane = lax.broadcasted_iota(jnp.int32, (kept.shape[0], LANES), 1)
    stats = jnp.zeros(lane.shape, F32)
    for i, number in enumerate(numbers):
        stats = jnp.where(lane == i, number, stats)
    packed[:, LATENT:] = stats.astype(jnp.int32).astype(jnp.int16)


def finish(packed, copies):
    chips, rows, _ = packed.shape
    stats = packed[:, :, LATENT:].astype(jnp.int32).astype(F32)
    level = from_parts(stats, 0)
    level = level - jnp.max(level, axis=0, keepdims=True)
    lower = jnp.sum(jnp.exp2(level) * from_parts(stats, 3), axis=0)
    factor = jnp.exp2(level + from_parts(stats, 6)) * (1.0 / STEPS)
    values = packed[:, :, :LATENT].astype(jnp.int32).astype(F32)
    upper = jnp.sum(factor * values, axis=0)
    final = (upper / lower).astype(jnp.bfloat16)
    copies[...] = jnp.broadcast_to(final[None], copies.shape)


def on_device(queries, latent_cache, lengths, offsets):
    requests, qtokens, heads, width = queries.shape
    positions = latent_cache.shape[1]
    rows = qtokens * heads
    chips = lax.axis_size(CHIPS)
    in_hbm = lambda a: pltpu.with_memory_space_constraint(a, pltpu.HBM)
    query = in_hbm(jnp.transpose(queries, (0, 1, 3, 2)))
    cache = in_hbm(jnp.transpose(latent_cache, (0, 2, 1)))
    lengths, offsets = in_hbm(lengths), in_hbm(offsets)
    swap = [(0, 1), (1, 0)]
    parts = positions // CHUNK
    limits = [pltpu.SMEM(lengths.shape, jnp.int32), pltpu.SMEM(offsets.shape, jnp.int32)]
    score = pltpu.VMEM((rows, positions), F32)
    triple = pltpu.VMEM((rows, LATENT + LANES), F32)
    cost = pl.CostEstimate(
        flops=2 * rows * positions * (width + LATENT),
        bytes_accessed=2 * positions * width,
        transcendentals=rows * positions,
    )

    lent, rows_q, keys = pl.pallas_call(
        lend,
        in_specs=[anywhere()] * 4,
        out_specs=[whole()] * 3,
        out_shape=[
            triple,
            pltpu.VMEM((rows, width), jnp.bfloat16),
            pltpu.VMEM((width, positions), jnp.bfloat16),
        ],
        scratch_shapes=[
            pltpu.VMEM(query.shape, jnp.bfloat16),
            pltpu.VMEM((rows, width), jnp.bfloat16),
            pltpu.VMEM((width, positions), jnp.bfloat16),
            score,
            *limits,
            pltpu.SemaphoreType.DMA((3,)),
            pltpu.SemaphoreType.DMA((parts,)),
            pltpu.SemaphoreType.DMA((parts,)),
        ],
        compiler_params=pltpu.CompilerParams(vmem_limit_bytes=32 * 2**20),
        cost_estimate=cost,
        name="lend",
    )(lengths, offsets, query, cache)
    lent = lax.ppermute(lent, CORE, swap)
    kept = pl.pallas_call(
        keep,
        in_specs=[anywhere(), anywhere(), whole(), whole()],
        out_specs=whole(),
        out_shape=triple,
        scratch_shapes=[score, *limits, pltpu.SemaphoreType.DMA((2,))],
        compiler_params=pltpu.CompilerParams(vmem_limit_bytes=32 * 2**20),
        cost_estimate=cost,
        name="keep",
    )(lengths, offsets, rows_q, keys)
    packed = pl.pallas_call(
        merge,
        in_specs=[whole()] * 2,
        out_specs=whole(),
        out_shape=pltpu.VMEM((rows, LATENT + LANES), jnp.int16),
        compiler_params=pltpu.CompilerParams(vmem_limit_bytes=8 * 2**20),
        name="merge",
    )(kept, lent)
    packed = packed.reshape(chips, rows // chips, LATENT + LANES)
    packed = lax.all_to_all(packed, CHIPS, 0, 0, tiled=True)
    copies = pl.pallas_call(
        finish,
        in_specs=[whole()],
        out_specs=whole(),
        out_shape=pltpu.VMEM((chips, rows // chips, LATENT), jnp.bfloat16),
        compiler_params=pltpu.CompilerParams(vmem_limit_bytes=8 * 2**20),
        name="finish",
    )(packed)
    mine = lax.all_to_all(copies, CHIPS, 0, 0, tiled=True).reshape(rows, LATENT)
    other = lax.ppermute(mine, CORE, swap)
    first = lax.axis_index(CORE) == 0
    both = jnp.where(first, jnp.stack([mine, other]), jnp.stack([other, mine]))
    return both.reshape(requests, qtokens, heads, LATENT)


def solution(mesh):
    torus = Mesh(mesh.devices.reshape(4, 4, 4, 2), SEQ)
    in_specs = (P(), P(None, SEQ, None), P(), P())
    return jax.shard_map(
        on_device, mesh=torus, in_specs=in_specs, out_specs=P(), check_vma=False
    )
```

time: 83.8 us -> 66 us (0.79)
  blocking collectives: 49.2 us -> 40.7 us
  Pallas kernels: 26.2 us -> 18 us
  local copies, waits for them, and re-layouts: 1.03 us -> 0 us
    pallas_call x4, Pallas kernels: 26.2 us -> 18 us  [the longest x1 8.91 us: on_device(): pl.pallas_call(lend, in_specs=[anywhere()] * 4, out_specs=[whole()] * 3,...]
    all_to_all x1, blocking collectives: 32.2 us -> 25.2 us  [on_device(): packed = lax.all_to_all(packed, CHIPS, 0, 0, tiled=True)]
    all_to_all x1, blocking collectives: 17 us -> 15.5 us  [on_device(): mine = lax.all_to_all(copies, CHIPS, 0, 0, tiled=True).reshape(rows, LATENT)]
    unnamed x4 -> x0, local copies, waits for them, and re-layouts: 1.03 us -> none
    ppermute x2 -> x1, starting transfers between devices: 1.73 us -> 1.46 us  [on_device(): lent = lax.ppermute(lent, CORE, swap)]
  transfers between devices with their start and end apart: 3 -> 2, of which waited for: 1 -> 1; matrix products, arithmetic and copies ran while one was open for 0% -> 0% of each run, Pallas kernels for 12% -> 12%
where the time goes in v2:
time: 66 us; the launch traced here: 65.8 us
  blocking collectives  40.7 us (62%)
  Pallas kernels  18 us (27%)
  starting transfers between devices  4.41 us (7%)
  waiting for transfers between devices  1.54 us (2%)
  other arithmetic  1.13 us (2%)
    all_to_all x1, blocking collectives, on_device(): packed = lax.all_to_all(packed, CHIPS, 0, 0, tiled=True)  25.2 us
    all_to_all x1, blocking collectives, on_device(): mine = lax.all_to_all(copies, CHIPS, 0, 0, tiled=True).reshape(rows, LATENT)  15.5 us
    pallas_call x1, Pallas kernels, on_device(): pl.pallas_call(lend, in_specs=[anywhere()] * 4, out_specs=[whole()] * 3,...  8.91 us
    pallas_call x1, Pallas kernels, on_device(): pl.pallas_call(keep, in_specs=[anywhere(), anywhere(), whole(), whole()],...  7.59 us
    ppermute x1, starting transfers between devices, on_device(): other = lax.ppermute(mine, CORE, swap)  2.95 us
    ppermute x1, waiting for transfers between devices, on_device(): other = lax.ppermute(mine, CORE, swap)  1.54 us
    ppermute x1, starting transfers between devices, on_device(): lent = lax.ppermute(lent, CORE, swap)  1.46 us
  transfers between devices with their start and end apart: 2, of which 1 were waited for; matrix products, arithmetic and copies ran while one was open for 0% of the time, Pallas kernels for 12%

profile of v2, /device:TPU:1, one launch (start us, length us, event | category | flops | bytes accessed | tf_op | source)
XLA Modules:
  0.0 65.8 jit_solution(14873295652526798068)
XLA Ops:
  0.0 8.9 %lend.1 = (f32[512,640]{1,0:T(8,128)S(1)}, bf16[512,576]{1,0:T(8,128)(2,1)S(1)}, bf16[576,4096]{1,0:T(8,128)(2,1)S(1)}) custom-call(s32[2]{0:T(128)} %lengths.3, s32[2,4]{1,0:T(2,128)} %offsets.3, bf16[2,4,576,128]{3,2,1,0:T(8,128)(2,1)} %bitcast.11, bf16[2,576,4096]{2,1,0:T(8,128)(2,1)} %bitcast.10), custom_call_target="tpu_custom_call" | custom-call | flops 4563402752 | bytes 4718592 | tf_op jit(solution)/shard_map/lend/pallas_call | solution.py:179
  8.9 1.5 %collective-permute-start = (f32[512,640]{1,0:T(8,128)S(1)}, f32[512,640]{1,0:T(8,128)S(1)}, u32[]{:S(2)}, u32[]{:S(2)}) collective-permute-start(f32[512,640]{1,0:T(8,128)S(1)} %get-tuple-element.10), channel_id=1, source_target_pairs={{0,1},{1,0},{2,3},{3,2},{4,5},{5,4},{6,7},{7,6},{8,9},{9,8},{10,11... | collective-permute-start | bytes 3932168 | tf_op jit(solution)/shard_map/ppermute | solution.py:202
  10.4 7.6 %keep.1.kept = f32[512,640]{1,0:T(8,128)S(1)} custom-call(s32[2]{0:T(128)} %lengths.3, s32[2,4]{1,0:T(2,128)} %offsets.3, bf16[512,576]{1,0:T(8,128)(2,1)S(1)} %get-tuple-element.8.rows_q, bf16[576,4096]{1,0:T(8,128)(2,1)S(1)} %get-tuple-element.9.keys), custom_call_target="tpu_custom_call" | custom-call | flops 4563402752 | bytes 4718592 | tf_op jit(solution)/shard_map/keep/pallas_call | solution.py:203
  18.0 0.0 collective-permute-done.lent
  18.0 1.0 %merge.1 = s16[512,640]{1,0:T(8,128)(2,1)S(1)} custom-call(f32[512,640]{1,0:T(8,128)S(1)} %keep.1.kept, f32[512,640]{1,0:T(8,128)S(1)} %collective-permute-done.lent), custom_call_target="tpu_custom_call" | custom-call | tf_op jit(solution)/shard_map/merge/pallas_call | solution.py:213
  19.0 25.2 %all_to_all.10.packed = s16[64,8,640]{2,1,0:T(8,128)(2,1)S(1)} all-to-all(s16[64,8,640]{2,1,0:T(8,128)(2,1)S(1)} %bitcast.6), channel_id=1, replica_groups=mesh['seq_0'=4,'seq_1'=4,'seq_2'=4,'seq_3'=2] {'seq_0','seq_1','seq_2'}, dimensions={0} | all-to-all | bytes 1310720 | tf_op jit(solution)/shard_map/all_to_all | solution.py:222
  44.2 0.5 finish.1
  44.7 15.5 %all_to_all.11 = bf16[64,8,512]{2,1,0:T(8,128)(2,1)S(1)} all-to-all(bf16[64,8,512]{2,1,0:T(8,128)(2,1)S(1)} %finish.1), channel_id=1, replica_groups=mesh['seq_0'=4,'seq_1'=4,'seq_2'=4,'seq_3'=2] {'seq_0','seq_1','seq_2'}, dimensions={0} | all-to-all | bytes 1048576 | tf_op jit(solution)/shard_map/all_to_all | solution.py:231
  60.2 2.9 %collective-permute-start.1 = (bf16[512,512]{1,0:T(8,128)(2,1)S(1)}, bf16[512,512]{1,0:T(8,128)(2,1)S(1)}, u32[]{:S(2)}, u32[]{:S(2)}) collective-permute-start(bf16[512,512]{1,0:T(8,128)(2,1)S(1)} %bitcast.7), channel_id=1, source_target_pairs={{0,1},{1,0},{2,3},{3,2},{4,5},{5,4},{6,7},{7,6},{8,9},{9,8},{10,11... | collective-permute-start | bytes 1572872 | tf_op jit(solution)/shard_map/ppermute | solution.py:232
  63.2 1.5 %collective-permute-done.1 = bf16[512,512]{1,0:T(8,128)(2,1)S(1)} collective-permute-done((bf16[512,512]{1,0:T(8,128)(2,1)S(1)}, bf16[512,512]{1,0:T(8,128)(2,1)S(1)}, u32[]{:S(2)}, u32[]{:S(2)}) %collective-permute-start.1) | collective-permute-done | bytes 524320 | tf_op jit(solution)/shard_map/ppermute | solution.py:232
  64.7 1.1 %maximum_select_fusion = bf16[2,4,128,512]{3,2,1,0:T(8,128)(2,1)} fusion(bf16[1,4,128,512]{3,2,1,0:T(8,128)(2,1)S(1)} %bitcast.9, bf16[1,4,128,512]{3,2,1,0:T(8,128)(2,1)S(1)} %bitcast.8, pred[]{:T(512)S(6)} %eq.3), kind=kLoop, calls=%fused_computation | loop fusion | flops 1572864 | bytes 2097153 | tf_op jit(solution)/shard_map/jit(_where)/select_n | solution.py:234
Async XLA Ops:
  8.9 9.1 %collective-permute-start = (f32[512,640]{1,0:T(8,128)S(1)}, f32[512,640]{1,0:T(8,128)S(1)}, u32[]{:S(2)}, u32[]{:S(2)}) collective-permute-start(f32[512,640]{1,0:T(8,128)S(1)} %get-tuple-element.10), channel_id=1, source_target_pairs={{0,1},{1,0},{2,3},{3,2},{4,5},{5,4},{6,7},{7,6},{8,9},{9,8},{10,11... | collective-permute-start | bytes 3932168 | tf_op jit(solution)/shard_map/ppermute | solution.py:202
  60.2 4.5 %collective-permute-start.1 = (bf16[512,512]{1,0:T(8,128)(2,1)S(1)}, bf16[512,512]{1,0:T(8,128)(2,1)S(1)}, u32[]{:S(2)}, u32[]{:S(2)}) collective-permute-start(bf16[512,512]{1,0:T(8,128)(2,1)S(1)} %bitcast.7), channel_id=1, source_target_pairs={{0,1},{1,0},{2,3},{3,2},{4,5},{5,4},{6,7},{7,6},{8,9},{9,8},{10,11... | collective-permute-start | bytes 1572872 | tf_op jit(solution)/shard_map/ppermute | solution.py:232

commit v3 on v2

v3 whole, which is shorter than its diff:
```python
import functools

import jax
import jax.numpy as jnp
from jax import lax
from jax.experimental import pallas as pl
from jax.experimental.pallas import tpu as pltpu
from jax.sharding import Mesh
from jax.sharding import PartitionSpec as P

LATENT = 512
CHIPS = ("seq_0", "seq_1", "seq_2")
CORE = "seq_3"
SEQ = (*CHIPS, CORE)
LANES = 128
SUBLANES = 8
HIDDEN = -1e30
LOG2_SCALE = 192.0 ** (-0.5) * 1.4426950408889634
CHUNK = 1024
STEPS = 32000.0
FINE = 32768.0
F32 = jnp.float32
whole = functools.partial(pl.BlockSpec, memory_space=pltpu.VMEM)
anywhere = functools.partial(pl.BlockSpec, memory_space=pltpu.HBM)


def scores(rows_q, keys, limits, score, peaks, ready):
    rows, positions = score.shape
    qtokens = limits.shape[0] // SUBLANES
    heads = rows // qtokens
    lane = lax.broadcasted_iota(jnp.int32, (heads, CHUNK), 1)
    peaks[...] = jnp.full((rows, LANES), HIDDEN, F32)
    for j in range(positions // CHUNK):
        part = slice(j * CHUNK, (j + 1) * CHUNK)
        ready(j)
        product = jnp.dot(rows_q[:, :LATENT], keys[:LATENT, part], preferred_element_type=F32)
        product += jnp.dot(rows_q[:, LATENT:], keys[LATENT:, part], preferred_element_type=F32)
        for t in range(qtokens):
            r = slice(t * heads, (t + 1) * heads)
            limit = limits[t * SUBLANES : t * SUBLANES + 1, :1] - j * CHUNK
            seen = jnp.where(lane < limit, product[r], HIDDEN)
            score[r, part] = seen
            top = peaks[r, :]
            for u in range(CHUNK // LANES):
                top = jnp.maximum(top, seen[:, u * LANES : (u + 1) * LANES])
            peaks[r, :] = top


def values(score, keys, peak, out):
    rows, positions = score.shape
    base = jnp.where(peak < 0.1 * HIDDEN, 0.0, peak)
    total = jnp.zeros((rows, LANES), F32)
    for j in range(positions // CHUNK):
        part = slice(j * CHUNK, (j + 1) * CHUNK)
        weight = jnp.exp2((score[:, part] - base) * LOG2_SCALE)
        for u in range(CHUNK // LANES):
            total = total + weight[:, u * LANES : (u + 1) * LANES]
        value = lax.dot_general(
            weight.astype(jnp.bfloat16),
            keys[:LATENT, part],
            (((1,), (1,)), ((), ())),
            preferred_element_type=F32,
        )
        if j == 0:
            out[...] = value
        else:
            out[...] += value
    return jnp.sum(total, axis=1, keepdims=True)


def lend(lengths, offsets, queries, cache, triple, next_q, next_keys, next_limits, query, rows_q, keys, score, limits, lens, offs, sems, key_sems, next_sems):
    positions = keys.shape[1]
    qtokens, _, heads = query.shape[1:]
    own = lax.axis_index(CORE)
    other = 1 - own
    start = lax.axis_index(SEQ) * positions

    def key_copy(request, into, own_sems, j):
        part = pl.ds(j * CHUNK, CHUNK)
        return pltpu.make_async_copy(cache.at[request, :, part], into.at[:, part], own_sems.at[j])

    parts = range(positions // CHUNK)
    first = [key_copy(other, keys, key_sems, j) for j in parts]
    later = [key_copy(own, next_keys, next_sems, j) for j in parts]
    query_copy = pltpu.make_async_copy(queries.at[other], query.at[0], sems.at[0])
    later_query = pltpu.make_async_copy(queries.at[own], query.at[1], sems.at[1])
    scalars = [
        pltpu.make_async_copy(lengths, lens, sems.at[2]),
        pltpu.make_async_copy(offsets, offs, sems.at[3]),
    ]
    for copy in (query_copy, first[0], *scalars, *first[1:], later_query, *later):
        copy.start()
    query_copy.wait()
    for t in range(qtokens):
        rows_q[t * heads : (t + 1) * heads, :] = query[0, t].T
    for copy in scalars:
        copy.wait()
    for request, into in ((other, limits), (own, next_limits)):
        for t in range(qtokens):
            limit = lens[request] - qtokens + 1 + offs[request, t] - start
            into[t * SUBLANES : (t + 1) * SUBLANES, :] = jnp.full((SUBLANES, LANES), limit, jnp.int32)
    stats = triple.at[:, LATENT:]
    scores(rows_q, keys, limits, score, stats, lambda j: first[j].wait())
    later_query.wait()
    for t in range(qtokens):
        next_q[t * heads : (t + 1) * heads, :] = query[1, t].T
    for copy in later:
        copy.wait()
    peak = jnp.max(stats[...], axis=1, keepdims=True)
    total = values(score, keys, peak, triple.at[:, :LATENT])
    left = lax.broadcasted_iota(jnp.int32, stats.shape, 1) < LANES // 2
    stats[...] = jnp.where(left, peak, total)


def look(rows_q, keys, limits, score, peaks):
    scores(rows_q, keys, limits, score, peaks, lambda j: None)


def in_parts(x):
    whole_part = jnp.round(x)
    rest = (x - whole_part) * FINE
    middle = jnp.round(rest)
    return [whole_part, middle, jnp.round((rest - middle) * FINE)]


def from_parts(stats, at):
    a, b, c = (stats[..., at + i : at + i + 1] for i in range(3))
    return a + (b + c * (1.0 / FINE)) * (1.0 / FINE)


def keep(score, peaks, keys, lent, packed, kept):
    half = LATENT + LANES // 2
    peak_a, peak_b = jnp.max(peaks[...], axis=1, keepdims=True), lent[:, LATENT : LATENT + 1]
    total_a = values(score, keys, peak_a, kept)
    peak = jnp.maximum(peak_a, peak_b)
    factor_a = jnp.exp2((peak_a - peak) * LOG2_SCALE)
    factor_b = jnp.exp2((peak_b - peak) * LOG2_SCALE)
    total = factor_a * total_a + factor_b * lent[:, half : half + 1]
    both = factor_a * kept[...] + factor_b * lent[:, :LATENT]
    largest = jnp.max(jnp.abs(both), axis=1, keepdims=True)
    largest = jnp.where(largest > 0.0, largest, 1.0)
    packed[:, :LATENT] = jnp.round(both * (STEPS / largest)).astype(jnp.int32).astype(jnp.int16)
    level = jnp.maximum(peak * LOG2_SCALE, -STEPS)
    numbers = [*in_parts(level), *in_parts(total), *in_parts(jnp.log2(largest))]
    lane = lax.broadcasted_iota(jnp.int32, (kept.shape[0], LANES), 1)
    stats = jnp.zeros(lane.shape, F32)
    for i, number in enumerate(numbers):
        stats = jnp.where(lane == i, number, stats)
    packed[:, LATENT:] = stats.astype(jnp.int32).astype(jnp.int16)


def finish(packed, copies):
    chips, rows, _ = packed.shape
    stats = packed[:, :, LATENT:].astype(jnp.int32).astype(F32)
    level = from_parts(stats, 0)
    level = level - jnp.max(level, axis=0, keepdims=True)
    lower = jnp.sum(jnp.exp2(level) * from_parts(stats, 3), axis=0)
    factor = jnp.exp2(level + from_parts(stats, 6)) * (1.0 / STEPS)
    values = packed[:, :, :LATENT].astype(jnp.int32).astype(F32)
    upper = jnp.sum(factor * values, axis=0)
    final = (upper / lower).astype(jnp.bfloat16)
    copies[...] = jnp.broadcast_to(final[None], copies.shape)


def place_own(rows, out, sem):
    copy = pltpu.make_async_copy(rows, out.at[lax.axis_index(CORE)], sem)
    copy.start()
    copy.wait()


def place_other(rows, half_done, out, sem):
    copy = pltpu.make_async_copy(rows, out.at[1 - lax.axis_index(CORE)], sem)
    copy.start()
    copy.wait()


def on_device(queries, latent_cache, lengths, offsets):
    requests, qtokens, heads, width = queries.shape
    positions = latent_cache.shape[1]
    rows = qtokens * heads
    chips = lax.axis_size(CHIPS)
    in_hbm = lambda a: pltpu.with_memory_space_constraint(a, pltpu.HBM)
    query = in_hbm(jnp.transpose(queries, (0, 1, 3, 2)))
    cache = in_hbm(jnp.transpose(latent_cache, (0, 2, 1)))
    lengths, offsets = in_hbm(lengths), in_hbm(offsets)
    swap = [(0, 1), (1, 0)]
    parts = positions // CHUNK
    score = pltpu.VMEM((rows, positions), F32)
    line = pltpu.VMEM((rows, width), jnp.bfloat16)
    key = pltpu.VMEM((width, positions), jnp.bfloat16)
    limit = pltpu.VMEM((qtokens * SUBLANES, LANES), jnp.int32)
    out = jax.ShapeDtypeStruct((requests, rows, LATENT), jnp.bfloat16)

    def cost(depth):
        return pl.CostEstimate(
            flops=2 * rows * positions * depth,
            bytes_accessed=2 * positions * width,
            transcendentals=rows * positions,
        )

    lent, rows_q, keys, limits = pl.pallas_call(
        lend,
        in_specs=[anywhere()] * 4,
        out_specs=[whole()] * 4,
        out_shape=[pltpu.VMEM((rows, LATENT + LANES), F32), line, key, limit],
        scratch_shapes=[
            pltpu.VMEM(query.shape, jnp.bfloat16),
            line,
            key,
            score,
            limit,
            pltpu.SMEM(lengths.shape, jnp.int32),
            pltpu.SMEM(offsets.shape, jnp.int32),
            pltpu.SemaphoreType.DMA((4,)),
            pltpu.SemaphoreType.DMA((parts,)),
            pltpu.SemaphoreType.DMA((parts,)),
        ],
        compiler_params=pltpu.CompilerParams(vmem_limit_bytes=32 * 2**20),
        cost_estimate=cost(width + LATENT),
        name="lend",
    )(lengths, offsets, query, cache)
    lent = lax.ppermute(lent, CORE, swap)
    score, peaks = pl.pallas_call(
        look,
        in_specs=[whole()] * 3,
        out_specs=[whole()] * 2,
        out_shape=[score, pltpu.VMEM((rows, LANES), F32)],
        compiler_params=pltpu.CompilerParams(vmem_limit_bytes=16 * 2**20),
        cost_estimate=cost(width),
        name="look",
    )(rows_q, keys, limits)
    packed = pl.pallas_call(
        keep,
        in_specs=[whole()] * 4,
        out_specs=whole(),
        out_shape=pltpu.VMEM((rows, LATENT + LANES), jnp.int16),
        scratch_shapes=[pltpu.VMEM((rows, LATENT), F32)],
        compiler_params=pltpu.CompilerParams(vmem_limit_bytes=16 * 2**20),
        cost_estimate=cost(LATENT),
        name="keep",
    )(score, peaks, keys, lent)
    packed = packed.reshape(chips, rows // chips, LATENT + LANES)
    packed = lax.all_to_all(packed, CHIPS, 0, 0, tiled=True)
    copies = pl.pallas_call(
        finish,
        in_specs=[whole()],
        out_specs=whole(),
        out_shape=pltpu.VMEM((chips, rows // chips, LATENT), jnp.bfloat16),
        compiler_params=pltpu.CompilerParams(vmem_limit_bytes=8 * 2**20),
        name="finish",
    )(packed)
    mine = lax.all_to_all(copies, CHIPS, 0, 0, tiled=True).reshape(rows, LATENT)
    other = lax.ppermute(mine, CORE, swap)
    both = pl.pallas_call(
        place_own,
        in_specs=[whole()],
        out_specs=anywhere(),
        out_shape=out,
        scratch_shapes=[pltpu.SemaphoreType.DMA(())],
        compiler_params=pltpu.CompilerParams(vmem_limit_bytes=2**20),
        cost_estimate=pl.CostEstimate(flops=10**7, bytes_accessed=4 * rows * LATENT, transcendentals=0),
        name="place_own",
    )(mine)
    both = pl.pallas_call(
        place_other,
        in_specs=[whole(), anywhere()],
        out_specs=anywhere(),
        out_shape=out,
        input_output_aliases={1: 0},
        scratch_shapes=[pltpu.SemaphoreType.DMA(())],
        compiler_params=pltpu.CompilerParams(vmem_limit_bytes=2**20),
        name="place_other",
    )(other, both)
    return both.reshape(requests, qtokens, heads, LATENT)


def solution(mesh):
    torus = Mesh(mesh.devices.reshape(4, 4, 4, 2), SEQ)
    in_specs = (P(), P(None, SEQ, None), P(), P())
    return jax.shard_map(
        on_device, mesh=torus, in_specs=in_specs, out_specs=P(), check_vma=False
    )
```

time: 66 us -> 64.5 us (0.977)
  other arithmetic: 1.13 us -> 0 us
  waiting for transfers between devices: 1.54 us -> 0.73 us
    select_n x1 -> x0, other arithmetic: 1.13 us -> none  [on_device(): both = jnp.where(first, jnp.stack([mine, other]), jnp.stack([other, mine]))]
    ppermute x1, waiting for transfers between devices: 1.54 us -> 0.73 us  [on_device(): other = lax.ppermute(mine, CORE, swap)]
    pallas_call x3 -> x5, Pallas kernels: 17.5 us -> 18 us  [the longest x1 9.11 us: on_device(): pl.pallas_call(lend, in_specs=[anywhere()] * 4, out_specs=[whole()] * 4,...]
  transfers between devices with their start and end apart: 2 -> 2, of which waited for: 1 -> 1; matrix products, arithmetic and copies ran while one was open for 0% -> 0% of each run, Pallas kernels for 12% -> 7%
where the time goes in v3:
time: 64.5 us; the launch traced here: 64.3 us
  blocking collectives  40.7 us (63%)
  Pallas kernels  18.5 us (29%)
  starting transfers between devices  4.39 us (7%)
  waiting for transfers between devices  0.73 us (1%)
    all_to_all x1, blocking collectives, on_device(): packed = lax.all_to_all(packed, CHIPS, 0, 0, tiled=True)  25.2 us
    all_to_all x1, blocking collectives, on_device(): mine = lax.all_to_all(copies, CHIPS, 0, 0, tiled=True).reshape(rows, LATENT)  15.5 us
    pallas_call x1, Pallas kernels, on_device(): pl.pallas_call(lend, in_specs=[anywhere()] * 4, out_specs=[whole()] * 4,...  9.11 us
    pallas_call x1, Pallas kernels, on_device(): pl.pallas_call(keep, in_specs=[whole()] * 4, out_specs=whole(), out_shape...  3.74 us
    pallas_call x1, Pallas kernels, on_device(): pl.pallas_call(look, in_specs=[whole()] * 3, out_specs=[whole()] * 2, out...  3.52 us
    ppermute x1, starting transfers between devices, on_device(): other = lax.ppermute(mine, CORE, swap)  2.95 us
    ppermute x1, starting transfers between devices, on_device(): lent = lax.ppermute(lent, CORE, swap)  1.45 us
  transfers between devices with their start and end apart: 2, of which 1 were waited for; matrix products, arithmetic and copies ran while one was open for 0% of the time, Pallas kernels for 7%

profile of v3, /device:TPU:1, one launch (start us, length us, event | category | flops | bytes accessed | tf_op | source)
XLA Modules:
  0.0 64.3 jit_solution(3598157050991617880)
XLA Ops:
  0.0 9.1 %lend.1 = (f32[512,640]{1,0:T(8,128)S(1)}, bf16[512,576]{1,0:T(8,128)(2,1)S(1)}, bf16[576,4096]{1,0:T(8,128)(2,1)S(1)}, s32[32,128]{1,0:T(8,128)S(1)}) custom-call(s32[2]{0:T(128)} %lengths.1, s32[2,4]{1,0:T(2,128)} %offsets.1, bf16[2,4,576,128]{3,2,1,0:T(8,128)(2,1)} %bitcast.9, bf16[2,576,4096]{2,1,0:T(8,128)(2,1)} %bitcast.8), custom_call_target="tpu_custom_call" | custom-call | flops 4563402752 | bytes 4718592 | tf_op jit(solution)/shard_map/lend/pallas_call | solution.py:201
  9.1 1.4 %collective-permute-start = (f32[512,640]{1,0:T(8,128)S(1)}, f32[512,640]{1,0:T(8,128)S(1)}, u32[]{:S(2)}, u32[]{:S(2)}) collective-permute-start(f32[512,640]{1,0:T(8,128)S(1)} %get-tuple-element.16), channel_id=1, source_target_pairs={{0,1},{1,0},{2,3},{3,2},{4,5},{5,4},{6,7},{7,6},{8,9},{9,8},{10,11... | collective-permute-start | bytes 3932168 | tf_op jit(solution)/shard_map/ppermute | solution.py:222
  10.6 3.5 %look.1 = (f32[512,4096]{1,0:T(8,128)S(1)}, f32[512,128]{1,0:T(8,128)S(1)}) custom-call(bf16[512,576]{1,0:T(8,128)(2,1)S(1)} %get-tuple-element.11.rows_q, bf16[576,4096]{1,0:T(8,128)(2,1)S(1)} %get-tuple-element.12.keys, s32[32,128]{1,0:T(8,128)S(1)} %get-tuple-element.13.limits), custom_call_target="tpu_custom_call" | custom-call | flops 2415919104 | bytes 4718592 | tf_op jit(solution)/shard_map/look/pallas_call | solution.py:223
  14.1 0.0 collective-permute-done.lent
  14.1 3.7 %keep.1 = s16[512,640]{1,0:T(8,128)(2,1)S(1)} custom-call(f32[512,4096]{1,0:T(8,128)S(1)} %get-tuple-element.14.score, f32[512,128]{1,0:T(8,128)S(1)} %get-tuple-element.15.peaks, bf16[576,4096]{1,0:T(8,128)(2,1)S(1)} %get-tuple-element.12.keys, f32[512,640]{1,0:T(8,128)S(1)} %collective-permute-done.lent), custom_call_target="tpu_custom_call" | custom-call | flops 2147483648 | bytes 4718592 | tf_op jit(solution)/shard_map/keep/pallas_call | solution.py:232
  17.9 25.2 %all_to_all.10.packed = s16[64,8,640]{2,1,0:T(8,128)(2,1)S(1)} all-to-all(s16[64,8,640]{2,1,0:T(8,128)(2,1)S(1)} %bitcast.5), channel_id=1, replica_groups=mesh['seq_0'=4,'seq_1'=4,'seq_2'=4,'seq_3'=2] {'seq_0','seq_1','seq_2'}, dimensions={0} | all-to-all | bytes 1310720 | tf_op jit(solution)/shard_map/all_to_all | solution.py:243
  43.1 0.5 finish.1
  43.5 15.5 %all_to_all.11 = bf16[64,8,512]{2,1,0:T(8,128)(2,1)S(1)} all-to-all(bf16[64,8,512]{2,1,0:T(8,128)(2,1)S(1)} %finish.1), channel_id=1, replica_groups=mesh['seq_0'=4,'seq_1'=4,'seq_2'=4,'seq_3'=2] {'seq_0','seq_1','seq_2'}, dimensions={0} | all-to-all | bytes 1048576 | tf_op jit(solution)/shard_map/all_to_all | solution.py:252
  59.1 2.9 %collective-permute-start.1 = (bf16[512,512]{1,0:T(8,128)(2,1)S(1)}, bf16[512,512]{1,0:T(8,128)(2,1)S(1)}, u32[]{:S(2)}, u32[]{:S(2)}) collective-permute-start(bf16[512,512]{1,0:T(8,128)(2,1)S(1)} %bitcast.6), channel_id=1, source_target_pairs={{0,1},{1,0},{2,3},{3,2},{4,5},{5,4},{6,7},{7,6},{8,9},{9,8},{10,11... | collective-permute-start | bytes 1572872 | tf_op jit(solution)/shard_map/ppermute | solution.py:253
  62.0 0.8 %place_own.1.half_done = bf16[2,512,512]{2,1,0:T(8,128)(2,1)} custom-call(bf16[512,512]{1,0:T(8,128)(2,1)S(1)} %bitcast.7), custom_call_target="tpu_custom_call" | custom-call | flops 10000000 | bytes 1048576 | tf_op jit(solution)/shard_map/place_own/pallas_call | solution.py:254
  62.8 0.7 %collective-permute-done.1.rows = bf16[512,512]{1,0:T(8,128)(2,1)S(1)} collective-permute-done((bf16[512,512]{1,0:T(8,128)(2,1)S(1)}, bf16[512,512]{1,0:T(8,128)(2,1)S(1)}, u32[]{:S(2)}, u32[]{:S(2)}) %collective-permute-start.1) | collective-permute-done | bytes 524320 | tf_op jit(solution)/shard_map/ppermute | solution.py:253
  63.5 0.8 %place_other.1 = bf16[2,512,512]{2,1,0:T(8,128)(2,1)} custom-call(bf16[512,512]{1,0:T(8,128)(2,1)S(1)} %collective-permute-done.1.rows, bf16[2,512,512]{2,1,0:T(8,128)(2,1)} %place_own.1.half_done), custom_call_target="tpu_custom_call", output_to_operand_aliasing={{}: (1, {})} | custom-call | tf_op jit(solution)/shard_map/place_other/pallas_call | solution.py:264
Async XLA Ops:
  9.1 5.0 %collective-permute-start = (f32[512,640]{1,0:T(8,128)S(1)}, f32[512,640]{1,0:T(8,128)S(1)}, u32[]{:S(2)}, u32[]{:S(2)}) collective-permute-start(f32[512,640]{1,0:T(8,128)S(1)} %get-tuple-element.16), channel_id=1, source_target_pairs={{0,1},{1,0},{2,3},{3,2},{4,5},{5,4},{6,7},{7,6},{8,9},{9,8},{10,11... | collective-permute-start | bytes 3932168 | tf_op jit(solution)/shard_map/ppermute | solution.py:222
  59.1 4.5 %collective-permute-start.1 = (bf16[512,512]{1,0:T(8,128)(2,1)S(1)}, bf16[512,512]{1,0:T(8,128)(2,1)S(1)}, u32[]{:S(2)}, u32[]{:S(2)}) collective-permute-start(bf16[512,512]{1,0:T(8,128)(2,1)S(1)} %bitcast.6), channel_id=1, source_target_pairs={{0,1},{1,0},{2,3},{3,2},{4,5},{5,4},{6,7},{7,6},{8,9},{9,8},{10,11... | collective-permute-start | bytes 1572872 | tf_op jit(solution)/shard_map/ppermute | solution.py:253

commit v4 on v3

--- a/solution.py
+++ b/solution.py
@@ -17,6 +17,8 @@
 HIDDEN = -1e30
 LOG2_SCALE = 192.0 ** (-0.5) * 1.4426950408889634
 CHUNK = 1024
+FIRST = 1024
+STEP = 256
 STEPS = 32000.0
 FINE = 32768.0
 F32 = jnp.float32
@@ -24,40 +26,46 @@
 anywhere = functools.partial(pl.BlockSpec, memory_space=pltpu.HBM)
 
 
-def scores(rows_q, keys, limits, score, peaks, ready):
-    rows, positions = score.shape
+def scores(rows_q, keys, limits, score, peaks, spans, ready):
+    rows = score.shape[0]
     qtokens = limits.shape[0] // SUBLANES
     heads = rows // qtokens
-    lane = lax.broadcasted_iota(jnp.int32, (heads, CHUNK), 1)
     peaks[...] = jnp.full((rows, LANES), HIDDEN, F32)
-    for j in range(positions // CHUNK):
-        part = slice(j * CHUNK, (j + 1) * CHUNK)
+    for j, (begin, size) in enumerate(spans):
+        part = slice(begin, begin + size)
+        lane = lax.broadcasted_iota(jnp.int32, (heads, size), 1)
         ready(j)
         product = jnp.dot(rows_q[:, :LATENT], keys[:LATENT, part], preferred_element_type=F32)
         product += jnp.dot(rows_q[:, LATENT:], keys[LATENT:, part], preferred_element_type=F32)
         for t in range(qtokens):
             r = slice(t * heads, (t + 1) * heads)
-            limit = limits[t * SUBLANES : t * SUBLANES + 1, :1] - j * CHUNK
+            limit = limits[t * SUBLANES : t * SUBLANES + 1, :1] - begin
             seen = jnp.where(lane < limit, product[r], HIDDEN)
             score[r, part] = seen
             top = peaks[r, :]
-            for u in range(CHUNK // LANES):
+            for u in range(size // LANES):
                 top = jnp.maximum(top, seen[:, u * LANES : (u + 1) * LANES])
             peaks[r, :] = top
 
 
 def values(score, keys, peak, out):
     rows, positions = score.shape
-    base = jnp.where(peak < 0.1 * HIDDEN, 0.0, peak)
+    base = jnp.broadcast_to(jnp.where(peak < 0.1 * HIDDEN, 0.0, peak), (rows, LANES))
     total = jnp.zeros((rows, LANES), F32)
-    for j in range(positions // CHUNK):
-        part = slice(j * CHUNK, (j + 1) * CHUNK)
-        weight = jnp.exp2((score[:, part] - base) * LOG2_SCALE)
-        for u in range(CHUNK // LANES):
-            total = total + weight[:, u * LANES : (u + 1) * LANES]
+
+    def weights(j, base, total):
+        cut = []
+        for u in range(j * STEP, (j + 1) * STEP, LANES):
+            weight = jnp.exp2((score[:, u : u + LANES] - base) * LOG2_SCALE)
+            total = total + weight
+            cut.append(weight.astype(jnp.bfloat16))
+        return jnp.concatenate(cut, axis=1), total
+
+    weight, total = weights(0, base, total)
+    for j in range(positions // STEP):
         value = lax.dot_general(
-            weight.astype(jnp.bfloat16),
-            keys[:LATENT, part],
+            weight,
+            keys[:LATENT, j * STEP : (j + 1) * STEP],
             (((1,), (1,)), ((), ())),
             preferred_element_type=F32,
         )
@@ -65,10 +73,12 @@
             out[...] = value
         else:
             out[...] += value
+        if (j + 1) * STEP < positions:
+            weight, total = weights(j + 1, base + value[:, :LANES] * 0.0, total)
     return jnp.sum(total, axis=1, keepdims=True)
 
 
-def lend(lengths, offsets, queries, cache, triple, next_q, next_keys, next_limits, query, rows_q, keys, score, limits, lens, offs, sems, key_sems, next_sems):
+def lend(lengths, offsets, queries, cache, triple, next_q, next_keys, next_limits, query, rows_q, keys, score, limits, lens, offs, sems, key_sems, next_sems, *, spans):
     positions = keys.shape[1]
     qtokens, _, heads = query.shape[1:]
     own = lax.axis_index(CORE)
@@ -76,10 +86,10 @@
     start = lax.axis_index(SEQ) * positions
 
     def key_copy(request, into, own_sems, j):
-        part = pl.ds(j * CHUNK, CHUNK)
+        part = pl.ds(*spans[j])
         return pltpu.make_async_copy(cache.at[request, :, part], into.at[:, part], own_sems.at[j])
 
-    parts = range(positions // CHUNK)
+    parts = range(len(spans))
     first = [key_copy(other, keys, key_sems, j) for j in parts]
     later = [key_copy(own, next_keys, next_sems, j) for j in parts]
     query_copy = pltpu.make_async_copy(queries.at[other], query.at[0], sems.at[0])
@@ -99,8 +109,8 @@
         for t in range(qtokens):
             limit = lens[request] - qtokens + 1 + offs[request, t] - start
             into[t * SUBLANES : (t + 1) * SUBLANES, :] = jnp.full((SUBLANES, LANES), limit, jnp.int32)
-    stats = triple.at[:, LATENT:]
-    scores(rows_q, keys, limits, score, stats, lambda j: first[j].wait())
+    stats = triple.at[:, LATENT : LATENT + LANES]
+    scores(rows_q, keys, limits, score, stats, spans, lambda j: first[j].wait())
     later_query.wait()
     for t in range(qtokens):
         next_q[t * heads : (t + 1) * heads, :] = query[1, t].T
@@ -108,19 +118,14 @@
         copy.wait()
     peak = jnp.max(stats[...], axis=1, keepdims=True)
     total = values(score, keys, peak, triple.at[:, :LATENT])
-    left = lax.broadcasted_iota(jnp.int32, stats.shape, 1) < LANES // 2
-    stats[...] = jnp.where(left, peak, total)
+    stats[...] = jnp.broadcast_to(peak, stats.shape)
+    triple[:, LATENT + LANES :] = jnp.broadcast_to(total, stats.shape)
 
 
 def look(rows_q, keys, limits, score, peaks):
-    scores(rows_q, keys, limits, score, peaks, lambda j: None)
-
-
-def in_parts(x):
-    whole_part = jnp.round(x)
-    rest = (x - whole_part) * FINE
-    middle = jnp.round(rest)
-    return [whole_part, middle, jnp.round((rest - middle) * FINE)]
+    positions = score.shape[1]
+    spans = [(i, CHUNK) for i in range(0, positions, CHUNK)]
+    scores(rows_q, keys, limits, score, peaks, spans, lambda j: None)
 
 
 def from_parts(stats, at):
@@ -128,24 +133,33 @@
     return a + (b + c * (1.0 / FINE)) * (1.0 / FINE)
 
 
-def keep(score, peaks, keys, lent, packed, kept):
-    half = LATENT + LANES // 2
-    peak_a, peak_b = jnp.max(peaks[...], axis=1, keepdims=True), lent[:, LATENT : LATENT + 1]
-    total_a = values(score, keys, peak_a, kept)
+def keep(score, peaks, keys, lent, packed, kept, scaled):
+    peak_a, peak_b = jnp.max(peaks[...], axis=1, keepdims=True), lent[:, LATENT : LATENT + LANES]
     peak = jnp.maximum(peak_a, peak_b)
     factor_a = jnp.exp2((peak_a - peak) * LOG2_SCALE)
     factor_b = jnp.exp2((peak_b - peak) * LOG2_SCALE)
-    total = factor_a * total_a + factor_b * lent[:, half : half + 1]
-    both = factor_a * kept[...] + factor_b * lent[:, :LATENT]
-    largest = jnp.max(jnp.abs(both), axis=1, keepdims=True)
-    largest = jnp.where(largest > 0.0, largest, 1.0)
-    packed[:, :LATENT] = jnp.round(both * (STEPS / largest)).astype(jnp.int32).astype(jnp.int16)
+    total = factor_b * lent[:, LATENT + LANES :]
+    blocks = range(0, LATENT, LANES)
+    for u in blocks:
+        scaled[:, u : u + LANES] = factor_b * lent[:, u : u + LANES]
+    total = total + factor_a * values(score, keys, peak_a, kept)
+    both = [factor_a * kept[:, u : u + LANES] + scaled[:, u : u + LANES] for u in blocks]
+    sizes = [jnp.abs(x) for x in both]
+    largest = jnp.maximum(jnp.maximum(sizes[0], sizes[1]), jnp.maximum(sizes[2], sizes[3]))
+    largest = jnp.max(largest, axis=1, keepdims=True)
+    largest = jnp.broadcast_to(jnp.where(largest > 0.0, largest, 1.0), peak.shape)
+    steps = STEPS / largest
+    for u, x in zip(blocks, both):
+        packed[:, u : u + LANES] = jnp.round(x * steps).astype(jnp.int32).astype(jnp.int16)
+    lane = lax.broadcasted_iota(jnp.int32, peak.shape, 1)
     level = jnp.maximum(peak * LOG2_SCALE, -STEPS)
-    numbers = [*in_parts(level), *in_parts(total), *in_parts(jnp.log2(largest))]
-    lane = lax.broadcasted_iota(jnp.int32, (kept.shape[0], LANES), 1)
-    stats = jnp.zeros(lane.shape, F32)
-    for i, number in enumerate(numbers):
-        stats = jnp.where(lane == i, number, stats)
+    number = jnp.where(lane < 3, level, jnp.where(lane < 6, total, jnp.log2(largest)))
+    whole_part = jnp.round(number)
+    rest = (number - whole_part) * FINE
+    middle = jnp.round(rest)
+    last = jnp.round((rest - middle) * FINE)
+    digit = lane % 3
+    stats = jnp.where(digit == 0, whole_part, jnp.where(digit == 1, middle, last))
     packed[:, LATENT:] = stats.astype(jnp.int32).astype(jnp.int16)
 
 
@@ -184,7 +198,7 @@
     cache = in_hbm(jnp.transpose(latent_cache, (0, 2, 1)))
     lengths, offsets = in_hbm(lengths), in_hbm(offsets)
     swap = [(0, 1), (1, 0)]
-    parts = positions // CHUNK
+    spans = [(0, FIRST), (FIRST, positions - FIRST)]
     score = pltpu.VMEM((rows, positions), F32)
     line = pltpu.VMEM((rows, width), jnp.bfloat16)
     key = pltpu.VMEM((width, positions), jnp.bfloat16)
@@ -199,10 +213,10 @@
         )
 
     lent, rows_q, keys, limits = pl.pallas_call(
-        lend,
+        functools.partial(lend, spans=spans),
         in_specs=[anywhere()] * 4,
         out_specs=[whole()] * 4,
-        out_shape=[pltpu.VMEM((rows, LATENT + LANES), F32), line, key, limit],
+        out_shape=[pltpu.VMEM((rows, LATENT + 2 * LANES), F32), line, key, limit],
         scratch_shapes=[
             pltpu.VMEM(query.shape, jnp.bfloat16),
             line,
@@ -212,8 +226,8 @@
             pltpu.SMEM(lengths.shape, jnp.int32),
             pltpu.SMEM(offsets.shape, jnp.int32),
             pltpu.SemaphoreType.DMA((4,)),
-            pltpu.SemaphoreType.DMA((parts,)),
-            pltpu.SemaphoreType.DMA((parts,)),
+            pltpu.SemaphoreType.DMA((len(spans),)),
+            pltpu.SemaphoreType.DMA((len(spans),)),
         ],
         compiler_params=pltpu.CompilerParams(vmem_limit_bytes=32 * 2**20),
         cost_estimate=cost(width + LATENT),
@@ -234,7 +248,7 @@
         in_specs=[whole()] * 4,
         out_specs=whole(),
         out_shape=pltpu.VMEM((rows, LATENT + LANES), jnp.int16),
-        scratch_shapes=[pltpu.VMEM((rows, LATENT), F32)],
+        scratch_shapes=[pltpu.VMEM((rows, LATENT), F32)] * 2,
         compiler_params=pltpu.CompilerParams(vmem_limit_bytes=16 * 2**20),
         cost_estimate=cost(LATENT),
         name="keep",

time: 64.5 us -> 62.8 us (0.974)
  Pallas kernels: 18.5 us -> 16.8 us
    pallas_call x1, Pallas kernels: 3.74 us -> 2.9 us  [on_device(): pl.pallas_call(keep, in_specs=[whole()] * 4, out_specs=whole(), out_shape...]
    pallas_call x1, Pallas kernels: 9.11 us -> 8.29 us  [on_device(): pl.pallas_call(functools.partial(lend, spans=spans), in_specs=[anywhere()...]
where the time goes in v4:
time: 62.8 us; the launch traced here: 62.7 us
  blocking collectives  40.7 us (65%)
  Pallas kernels  16.8 us (27%)
  starting transfers between devices  4.42 us (7%)
  waiting for transfers between devices  0.73 us (1%)
    all_to_all x1, blocking collectives, on_device(): packed = lax.all_to_all(packed, CHIPS, 0, 0, tiled=True)  25.2 us
    all_to_all x1, blocking collectives, on_device(): mine = lax.all_to_all(copies, CHIPS, 0, 0, tiled=True).reshape(rows, LATENT)  15.5 us
    pallas_call x1, Pallas kernels, on_device(): pl.pallas_call(functools.partial(lend, spans=spans), in_specs=[anywhere()...  8.29 us
    pallas_call x1, Pallas kernels, on_device(): pl.pallas_call(look, in_specs=[whole()] * 3, out_specs=[whole()] * 2, out...  3.51 us
    ppermute x1, starting transfers between devices, on_device(): other = lax.ppermute(mine, CORE, swap)  2.95 us
    pallas_call x1, Pallas kernels, on_device(): pl.pallas_call(keep, in_specs=[whole()] * 4, out_specs=whole(), out_shape...  2.9 us
    ppermute x1, starting transfers between devices, on_device(): lent = lax.ppermute(lent, CORE, swap)  1.47 us
  transfers between devices with their start and end apart: 2, of which 1 were waited for; matrix products, arithmetic and copies ran while one was open for 0% of the time, Pallas kernels for 7%

profile of v4, /device:TPU:1, one launch (start us, length us, event | category | flops | bytes accessed | tf_op | source)
XLA Modules:
  0.0 62.7 jit_solution(5188226904704920961)
XLA Ops:
  0.0 8.3 %lend.1 = (f32[512,768]{1,0:T(8,128)S(1)}, bf16[512,576]{1,0:T(8,128)(2,1)S(1)}, bf16[576,4096]{1,0:T(8,128)(2,1)S(1)}, s32[32,128]{1,0:T(8,128)S(1)}) custom-call(s32[2]{0:T(128)} %lengths.1, s32[2,4]{1,0:T(2,128)} %offsets.1, bf16[2,4,576,128]{3,2,1,0:T(8,128)(2,1)} %bitcast.9, bf16[2,576,4096]{2,1,0:T(8,128)(2,1)} %bitcast.8), custom_call_target="tpu_custom_call" | custom-call | flops 4563402752 | bytes 4718592 | tf_op jit(solution)/shard_map/lend/pallas_call | solution.py:215
  8.3 1.5 %collective-permute-start = (f32[512,768]{1,0:T(8,128)S(1)}, f32[512,768]{1,0:T(8,128)S(1)}, u32[]{:S(2)}, u32[]{:S(2)}) collective-permute-start(f32[512,768]{1,0:T(8,128)S(1)} %get-tuple-element.16), channel_id=1, source_target_pairs={{0,1},{1,0},{2,3},{3,2},{4,5},{5,4},{6,7},{7,6},{8,9},{9,8},{10,11... | collective-permute-start | bytes 4718600 | tf_op jit(solution)/shard_map/ppermute | solution.py:236
  9.8 3.5 %look.1 = (f32[512,4096]{1,0:T(8,128)S(1)}, f32[512,128]{1,0:T(8,128)S(1)}) custom-call(bf16[512,576]{1,0:T(8,128)(2,1)S(1)} %get-tuple-element.11.rows_q, bf16[576,4096]{1,0:T(8,128)(2,1)S(1)} %get-tuple-element.12.keys, s32[32,128]{1,0:T(8,128)S(1)} %get-tuple-element.13.limits), custom_call_target="tpu_custom_call" | custom-call | flops 2415919104 | bytes 4718592 | tf_op jit(solution)/shard_map/look/pallas_call | solution.py:237
  13.3 0.0 collective-permute-done.lent
  13.3 2.9 %keep.1 = s16[512,640]{1,0:T(8,128)(2,1)S(1)} custom-call(f32[512,4096]{1,0:T(8,128)S(1)} %get-tuple-element.14.score, f32[512,128]{1,0:T(8,128)S(1)} %get-tuple-element.15.peaks, bf16[576,4096]{1,0:T(8,128)(2,1)S(1)} %get-tuple-element.12.keys, f32[512,768]{1,0:T(8,128)S(1)} %collective-permute-done.lent), custom_call_target="tpu_custom_call" | custom-call | flops 2147483648 | bytes 4718592 | tf_op jit(solution)/shard_map/keep/pallas_call | solution.py:246
  16.2 25.2 %all_to_all.10.packed = s16[64,8,640]{2,1,0:T(8,128)(2,1)S(1)} all-to-all(s16[64,8,640]{2,1,0:T(8,128)(2,1)S(1)} %bitcast.5), channel_id=1, replica_groups=mesh['seq_0'=4,'seq_1'=4,'seq_2'=4,'seq_3'=2] {'seq_0','seq_1','seq_2'}, dimensions={0} | all-to-all | bytes 1310720 | tf_op jit(solution)/shard_map/all_to_all | solution.py:257
  41.4 0.5 finish.1
  41.9 15.5 %all_to_all.11 = bf16[64,8,512]{2,1,0:T(8,128)(2,1)S(1)} all-to-all(bf16[64,8,512]{2,1,0:T(8,128)(2,1)S(1)} %finish.1), channel_id=1, replica_groups=mesh['seq_0'=4,'seq_1'=4,'seq_2'=4,'seq_3'=2] {'seq_0','seq_1','seq_2'}, dimensions={0} | all-to-all | bytes 1048576 | tf_op jit(solution)/shard_map/all_to_all | solution.py:266
  57.4 2.9 %collective-permute-start.1 = (bf16[512,512]{1,0:T(8,128)(2,1)S(1)}, bf16[512,512]{1,0:T(8,128)(2,1)S(1)}, u32[]{:S(2)}, u32[]{:S(2)}) collective-permute-start(bf16[512,512]{1,0:T(8,128)(2,1)S(1)} %bitcast.6), channel_id=1, source_target_pairs={{0,1},{1,0},{2,3},{3,2},{4,5},{5,4},{6,7},{7,6},{8,9},{9,8},{10,11... | collective-permute-start | bytes 1572872 | tf_op jit(solution)/shard_map/ppermute | solution.py:267
  60.3 0.8 %place_own.1.half_done = bf16[2,512,512]{2,1,0:T(8,128)(2,1)} custom-call(bf16[512,512]{1,0:T(8,128)(2,1)S(1)} %bitcast.7), custom_call_target="tpu_custom_call" | custom-call | flops 10000000 | bytes 1048576 | tf_op jit(solution)/shard_map/place_own/pallas_call | solution.py:268
  61.1 0.7 %collective-permute-done.1.rows = bf16[512,512]{1,0:T(8,128)(2,1)S(1)} collective-permute-done((bf16[512,512]{1,0:T(8,128)(2,1)S(1)}, bf16[512,512]{1,0:T(8,128)(2,1)S(1)}, u32[]{:S(2)}, u32[]{:S(2)}) %collective-permute-start.1) | collective-permute-done | bytes 524320 | tf_op jit(solution)/shard_map/ppermute | solution.py:267
  61.9 0.8 %place_other.1 = bf16[2,512,512]{2,1,0:T(8,128)(2,1)} custom-call(bf16[512,512]{1,0:T(8,128)(2,1)S(1)} %collective-permute-done.1.rows, bf16[2,512,512]{2,1,0:T(8,128)(2,1)} %place_own.1.half_done), custom_call_target="tpu_custom_call", output_to_operand_aliasing={{}: (1, {})} | custom-call | tf_op jit(solution)/shard_map/place_other/pallas_call | solution.py:278
Async XLA Ops:
  8.3 5.0 %collective-permute-start = (f32[512,768]{1,0:T(8,128)S(1)}, f32[512,768]{1,0:T(8,128)S(1)}, u32[]{:S(2)}, u32[]{:S(2)}) collective-permute-start(f32[512,768]{1,0:T(8,128)S(1)} %get-tuple-element.16), channel_id=1, source_target_pairs={{0,1},{1,0},{2,3},{3,2},{4,5},{5,4},{6,7},{7,6},{8,9},{9,8},{10,11... | collective-permute-start | bytes 4718600 | tf_op jit(solution)/shard_map/ppermute | solution.py:236
  57.4 4.5 %collective-permute-start.1 = (bf16[512,512]{1,0:T(8,128)(2,1)S(1)}, bf16[512,512]{1,0:T(8,128)(2,1)S(1)}, u32[]{:S(2)}, u32[]{:S(2)}) collective-permute-start(bf16[512,512]{1,0:T(8,128)(2,1)S(1)} %bitcast.6), channel_id=1, source_target_pairs={{0,1},{1,0},{2,3},{3,2},{4,5},{5,4},{6,7},{7,6},{8,9},{9,8},{10,11... | collective-permute-start | bytes 1572872 | tf_op jit(solution)/shard_map/ppermute | solution.py:267
